TPU v7x, 32 devices: a 4x4x1 block of a 4x4x8 slice. The times are simulated.
32 devices in a mesh: rep: 2 (over z, core), dp: 16 (over x, y).
Axes of the slice: x: 4, y: 4, z: 1, core: 2. Of those that a mesh axis runs over, the one named last changes fastest.
The devices are a block of a 4x4x8 slice.
Arguments:
- x: bfloat16 [32, 2048, 512], P(('rep', 'dp')), parts along dimension 0
- dy: bfloat16 [32, 2048, 512], P(('rep', 'dp')), parts along dimension 0
- w_gate: bfloat16 [2, 512, 3072], replicated
- w_up: bfloat16 [2, 512, 3072], replicated
- w_down: bfloat16 [2, 3072, 512], replicated
- m_w_gate: float32 [2, 512, 3072], replicated
- m_w_up: float32 [2, 512, 3072], replicated
- m_w_down: float32 [2, 3072, 512], replicated
- v_w_gate: float32 [2, 512, 3072], replicated
- v_w_up: float32 [2, 512, 3072], replicated
- v_w_down: float32 [2, 3072, 512], replicated
Outputs:
- output 1: bfloat16 [4, 512, 3072], P('rep'), parts along dimension 0
- output 2: bfloat16 [4, 512, 3072], P('rep'), parts along dimension 0
- output 3: bfloat16 [4, 3072, 512], P('rep'), parts along dimension 0
- output 4: float32 [4, 512, 3072], P('rep'), parts along dimension 0
- output 5: float32 [4, 512, 3072], P('rep'), parts along dimension 0
- output 6: float32 [4, 3072, 512], P('rep'), parts along dimension 0
- output 7: float32 [4, 512, 3072], P('rep'), parts along dimension 0
- output 8: float32 [4, 512, 3072], P('rep'), parts along dimension 0
- output 9: float32 [4, 3072, 512], P('rep'), parts along dimension 0
There are 2 independent parts. A program takes and returns all parts, laid end to end along the dimension named above; an argument that names none is the same for every part.
All inputs are finite; a program needn't handle non-finite values.
Results may differ from a plain program's by a relative error of at most 0.022.
Values are sent between devices in bfloat16 or wider.
A program may use at most 768 MiB of HBM per device.

v0:
```python
import jax
import jax.numpy as jnp
from jax import lax
from jax.sharding import PartitionSpec as P

NAMES = ("w_gate", "w_up", "w_down")


def matmul(a, w):
    return jnp.dot(a, w, preferred_element_type=jnp.float32).astype(jnp.bfloat16)


def normed(h):
    wide = h.astype(jnp.float32)
    scale = lax.rsqrt(jnp.mean(wide**2, -1, keepdims=True) + 1e-6)
    return (wide * scale).astype(jnp.bfloat16)


def layer(h, w):
    a = normed(h)
    gate = jnp.dot(a, w["w_gate"], preferred_element_type=jnp.float32)
    up = jnp.dot(a, w["w_up"], preferred_element_type=jnp.float32)
    return h + matmul((jax.nn.silu(gate) * up).astype(jnp.bfloat16), w["w_down"])


def adamw(w, m, v, g):
    m = 0.9 * m + 0.1 * g
    v = 0.95 * v + 0.05 * g * g
    step = m * lax.rsqrt(v + 1e-8) + 0.1 * w
    return (w - 0.02 * step).astype(jnp.bfloat16), m, v


def solution(mesh):
    def step(x, dy, *arrays):
        weights, m, v = (arrays[i : i + 3] for i in (0, 3, 6))
        layers = weights[0].shape[0]
        h, kept = x[0], []
        for number in range(layers):
            kept.append(h)
            h = layer(h, {name: w[number] for name, w in zip(NAMES, weights, strict=True)})
        by_h, summed = dy[0], [None] * layers
        for number in reversed(range(layers)):
            _, back = jax.vjp(lambda w, h: layer(h, w), {name: w[number] for name, w in zip(NAMES, weights, strict=True)}, kept[number])
            by_w, by_h = back(by_h)
            summed[number] = [lax.psum(by_w[name], "dp") for name in NAMES]
        gradients = [jnp.stack([summed[number][i] for number in range(layers)]).astype(jnp.float32) for i in range(3)]
        new = [adamw(w.astype(jnp.float32), m, v, g) for w, m, v, g in zip(weights, m, v, gradients, strict=True)]
        return tuple(one[which] for which in range(3) for one in new)

    return jax.shard_map(
        step,
        mesh=mesh,
        in_specs=(P(("rep", "dp"), None, None),) * 2 + (P(None, None, None),) * 9,
        out_specs=(P("rep", None, None),) * 9,
        check_vma=False,
    )
```

profile of v0, /device:TPU:97, one launch (start us, length us, event | category | flops | bytes accessed | tf_op | source)
XLA Modules:
  0.0 581.3 jit_solution(1706984565654312533)
XLA Ops:
  7.2 0.1 all-reduce.3.cloned.1.call-start
  7.3 2.9 copy.20
  10.2 0.0 copy-start
  10.2 0.5 fusion.37
  10.7 0.0 copy-start.10
  10.7 4.2 copy.21
  14.8 0.0 copy-start.4
  14.8 11.9 %convolution_convert_fusion.1 = bf16[2048,3072]{1,0:T(8,128)(2,1)} fusion(bf16[2,3072,512]{2,1,0:T(8,128)(2,1)} %param.15, bf16[1,2048,512]{2,1,0:T(8,128)(2,1)} %param.12), kind=kOutput, calls=%fused_computation.52 | convolution fusion | flops 6448742400 | bytes 17825792 | tf_op jit(solution)/shard_map/transpose(jvp())/dot_general | solution.py:10
  26.7 0.0 copy-done.4
  26.7 13.6 %fusion.65 = f32[2048,3072]{1,0:T(8,128)} fusion(bf16[2,512,3072]{2,1,0:T(8,128)(2,1)} %param.13, bf16[1,2048,512]{2,1,0:T(8,128)(2,1)S(1)} %copy-done.4, f32[2048]{0:T(1024)S(1)} %add_rsqrt_fusion), kind=kOutput, calls=%fused_computation.96 | convolution fusion | flops 6445596672 | bytes 30416896 | tf_op jit(solution)/shard_map/dot_general | solution.py:21
  40.4 0.0 copy-done.10
  40.4 24.7 %multiply_convert_fusion.1 = (bf16[2048,3072]{1,0:T(8,128)(2,1)}, f32[2048,3072]{1,0:T(8,128)}) fusion(f32[2048,3072]{1,0:T(8,128)} %fusion.65, bf16[2,512,3072]{2,1,0:T(8,128)(2,1)} %param.14, bf16[1,2048,512]{2,1,0:T(8,128)(2,1)} %param.11, f32[2048]{0:T(1024)S(1)} %add_rsqrt_fusion), kind=kOutput, calls=%fused_computation.17 | convolution fusion | flops 6483345408 | bytes 68165632 | tf_op jit(solution)/shard_map/dot_general | solution.py:22
  65.0 0.0 copy-done
  65.0 11.0 %fusion.41 = (f32[2048]{0:T(1024)S(1)}, bf16[2048,512]{0,1:T(8,128)(2,1)S(1)}) fusion(bf16[2048,3072]{1,0:T(8,128)(2,1)} %get-tuple-element.24, bf16[2,3072,512]{2,1,0:T(8,128)(2,1)} %param.15, bf16[1,2048,512]{1,2,0:T(8,128)(2,1)S(1)} %copy.20), kind=kOutput, calls=%fused_computation.73 | convolution fusion | flops 6447691776 | bytes 19931136 | tf_op jit(solution)/shard_map/dot_general | solution.py:10
  76.0 0.0 copy-start.8
  76.0 0.0 copy-start.6
  76.1 0.6 copy-done.8
  76.6 0.7 copy-done.6
  77.4 13.6 %fusion.52 = f32[2048,3072]{1,0:T(8,128)} fusion(bf16[2,512,3072]{2,1,0:T(8,128)(2,1)} %param.14, bf16[2048,512]{0,1:T(8,128)(2,1)S(1)} %get-tuple-element.27, f32[2048]{0:T(1024)S(1)} %fusion.103), kind=kOutput, calls=%fused_computation.83 | convolution fusion | flops 6445596672 | bytes 30416896 | tf_op jit(solution)/shard_map/jvp()/dot_general | solution.py:22
  91.0 36.7 %fusion.2 = (bf16[2048,3072]{1,0:T(8,128)(2,1)}, f32[2048,3072]{1,0:T(8,128)}) fusion(f32[2048,3072]{1,0:T(8,128)} %fusion.52, bf16[2048,3072]{1,0:T(8,128)(2,1)} %convolution_convert_fusion.1, bf16[2,512,3072]{2,1,0:T(8,128)(2,1)} %param.13, bf16[2048,512]{0,1:T(8,128)(2,1)} %copy-done.6, f32[2048]{0:T(1024)S(1)} %fusion.103), kind=kOutput, calls=%fused_computation.8 | convolution fusion | flops 6521094144 | bytes 80748544 | tf_op jit(solution)/shard_map/jvp()/dot_general | solution.py:21
  127.7 0.0 copy-start.5
  127.7 18.1 %fusion.76 = bf16[2048,512]{0,1:T(8,128)(2,1)} fusion(bf16[2048,3072]{1,0:T(8,128)(2,1)} %convolution_convert_fusion.1, bf16[2,512,3072]{2,1,0:T(8,128)(2,1)} %param.14, f32[2048,3072]{1,0:T(8,128)} %get-tuple-element.29), kind=kOutput, calls=%fused_computation.103 | convolution fusion | flops 6481248256 | bytes 42991616 | tf_op jit(solution)/shard_map/transpose(jvp())/dot_general | solution.py:22
  145.8 0.0 copy-done.5
  145.8 0.0 copy-start.3
  145.8 19.9 %fusion.48 = bf16[1,3072,512]{2,1,0:T(8,128)(2,1)} fusion(f32[2048,3072]{1,0:T(8,128)} %fusion.52, bf16[1,2048,512]{2,1,0:T(8,128)(2,1)S(1)} %copy-done.5, f32[2048,3072]{1,0:T(8,128)} %get-tuple-element.29), kind=kOutput, calls=%fused_computation.81 | convolution fusion | flops 6481772544 | bytes 55574528 | tf_op jit(solution)/shard_map/transpose(jvp())/dot_general | solution.py:10
  165.7 0.0 copy-done.3
  165.7 0.0 copy-start.9
  165.7 0.0 copy-start.2
  165.7 0.0 copy-start.7
  165.7 10.7 %fusion.43 = (f32[2048]{0:T(1024)S(1)}, bf16[2048,512]{0,1:T(8,128)(2,1)S(1)}) fusion(bf16[2048,512]{0,1:T(8,128)(2,1)} %copy-done.6, bf16[2048,512]{0,1:T(8,128)(2,1)} %fusion.76, bf16[2048,3072]{1,0:T(8,128)(2,1)} %get-tuple-element.28, bf16[2,512,3072]{2,1,0:T(8,128)(2,1)S(1)} %copy-done.3), kind=kOutput, calls=%fused_computation.75 | convolution fusion | flops 6447691776 | bytes 22028288 | tf_op jit(solution)/shard_map/transpose(jvp())/dot_general | solution.py:21
  176.4 0.0 copy-done.9
  176.4 0.0 copy-done.2
  176.4 0.0 copy-done.7
  176.4 0.0 slice-start.2
  176.4 1.4 fusion.92
  177.8 0.0 slice-start.3
  177.8 11.3 %fusion.44 = bf16[1,3072,512]{2,1,0:T(8,128)(2,1)} fusion(bf16[2048,3072]{1,0:T(8,128)(2,1)} %get-tuple-element.24, bf16[2048,512]{0,1:T(8,128)(2,1)S(1)} %fusion.92), kind=kOutput, calls=%fused_computation.77 | convolution fusion | flops 6444023808 | bytes 17825792 | tf_op jit(solution)/shard_map/transpose(jvp())/dot_general | solution.py:10
  189.1 0.0 slice-done.2
  189.1 0.0 slice-done.3
  189.1 9.8 %convolution_convert_fusion = bf16[2048,3072]{1,0:T(8,128)(2,1)} fusion(bf16[2048,512]{0,1:T(8,128)(2,1)S(1)} %fusion.92, bf16[2,3072,512]{2,1,0:T(8,128)(2,1)S(1)} %bitcast.83), kind=kOutput, calls=%fused_computation.51 | convolution fusion | flops 6448742400 | bytes 17825792 | tf_op jit(solution)/shard_map/transpose(jvp())/dot_general | solution.py:10
  198.9 17.6 %fusion.46 = bf16[1,512,3072]{2,1,0:T(8,128)(2,1)} fusion(bf16[2048,3072]{1,0:T(8,128)(2,1)} %convolution_convert_fusion.1, bf16[2048,512]{0,1:T(8,128)(2,1)S(1)} %copy-done.7, f32[2048]{0:T(1024)S(1)} %fusion.103, f32[2048,3072]{1,0:T(8,128)} %get-tuple-element.29), kind=kOutput, calls=%fused_computation.79 | convolution fusion | flops 6484918272 | bytes 42999808 | tf_op jit(solution)/shard_map/transpose(jvp())/dot_general | solution.py:22
  216.5 0.0 copy-start.1
  216.5 0.0 copy-start.11
  216.5 13.2 %fusion.47 = bf16[1,512,3072]{2,1,0:T(8,128)(2,1)} fusion(bf16[2048,3072]{1,0:T(8,128)(2,1)} %get-tuple-element.28, bf16[2048,512]{0,1:T(8,128)(2,1)} %copy-done.6, f32[2048]{0:T(1024)S(1)} %fusion.103), kind=kOutput, calls=%fused_computation.80 | convolution fusion | flops 6445596672 | bytes 17833984 | tf_op jit(solution)/shard_map/transpose(jvp())/dot_general | solution.py:21
  229.7 0.0 copy-done.1
  229.7 0.0 copy-done.11
  229.7 17.4 %fusion.45 = bf16[1,512,3072]{2,1,0:T(8,128)(2,1)} fusion(bf16[2048,3072]{1,0:T(8,128)(2,1)} %convolution_convert_fusion, f32[2048,3072]{1,0:T(8,128)} %fusion.65, bf16[1,2048,512]{1,2,0:T(8,128)(2,1)S(1)} %copy-done.1, f32[2048]{0:T(1024)S(1)} %copy-done.11), kind=kOutput, calls=%fused_computation.78 | convolution fusion | flops 6484918272 | bytes 42999808 | tf_op jit(solution)/shard_map/transpose(jvp())/dot_general | solution.py:22
  247.1 24.7 %fusion.49 = bf16[1,512,3072]{2,1,0:T(8,128)(2,1)} fusion(f32[2048,3072]{1,0:T(8,128)} %fusion.65, f32[2048,3072]{1,0:T(8,128)} %get-tuple-element.25, bf16[2048,3072]{1,0:T(8,128)(2,1)} %convolution_convert_fusion, bf16[1,2048,512]{1,2,0:T(8,128)(2,1)S(1)} %copy-done.1, f32[2048]{0:T(1024)S(1)} %copy-done.11), kind=kOutput, calls=%fused_computation.82 | convolution fusion | flops 6516375552 | bytes 68165632 | tf_op jit(solution)/shard_map/transpose(jvp())/dot_general | solution.py:21
  271.8 0.0 slice-start
  271.8 0.1 all-reduce.3.cloned.1.call-update
  271.9 234.4 %all-reduce.3.cloned.1.call-done = (bf16[1,512,3072]{2,1,0:T(8,128)(2,1)}, bf16[1,512,3072]{2,1,0:T(8,128)(2,1)}, bf16[1,512,3072]{2,1,0:T(8,128)(2,1)}, bf16[1,...) async-done(((bf16[1,512,3072]{2,1,0:T(8,128)(2,1)}, bf16[1,512,3072]{2,1,0:T(8,128)(2,1)}, bf16[1,512,3072]{2,1,0:T(8,128)(2,1)}, ...) | async-done | bytes 18874384 | tf_op jit(solution)/shard_map/psum | solution.py:45
  506.2 0.0 slice-start.1
  506.2 25.7 %fusion.23 = (bf16[2,3072,512]{2,1,0:T(8,128)(2,1)}, f32[2,3072,512]{2,1,0:T(8,128)}, f32[2,3072,512]{2,1,0:T(8,128)}) fusion(bf16[2,3072,512]{2,1,0:T(8,128)(2,1)} %param.15, bf16[1,3072,512]{2,1,0:T(8,128)(2,1)} %get-tuple-element.13, bf16[1,3072,512]{2,1,0:T(8,128)(2,1)} %get-tuple-element.14, f32[2,3072,512]{2,1,0:T(8,128)} %param.21, ...), kind=kLoop, calls=%fused_computation.44 | loop fusion | flops 59768832 | bytes 69206016 | tf_op jit(solution)/shard_map/convert_element_type | solution.py:30
  531.9 0.0 slice-done
  531.9 0.0 slice-done.1
  531.9 42.0 %fusion.15 = (bf16[2,512,3072]{2,1,0:T(8,128)(2,1)}, f32[2,512,3072]{2,1,0:T(8,128)}, f32[2,512,3072]{2,1,0:T(8,128)}, bf16[2,512,3072]{2,1,0:T(8,128)(2,1)}, f3...) fusion(bf16[2,512,3072]{2,1,0:T(8,128)(2,1)S(1)} %bitcast.81, bf16[1,512,3072]{2,1,0:T(8,128)(2,1)} %get-tuple-element.9, ...), kind=kLoop, calls=%fused_computation.36 | loop fusion | flops 119537664 | bytes 138412032 | tf_op jit(solution)/shard_map/convert_element_type | solution.py:30
  (5 shorter events, 0.0 us)
Async XLA Ops:
  7.2 499.1 %all-reduce.3.cloned.1.call-start = ((), (), s32[]{:S(2)}) async-start(), calls=%async_computation | async-start | bytes 37748736 | tf_op jit(solution)/shard_map/psum | solution.py:45
  10.2 54.8 %copy-start = (bf16[1,2048,512]{1,2,0:T(8,128)(2,1)}, bf16[1,2048,512]{1,2,0:T(8,128)(2,1)S(1)}, u32[]{:S(2)}) copy-start(bf16[1,2048,512]{1,2,0:T(8,128)(2,1)S(1)} %copy.20) | copy-start | bytes 6291460
  10.7 29.7 %copy-start.10 = (f32[2048]{0:T(1024)}, f32[2048]{0:T(1024)S(1)}, u32[]{:S(2)}) copy-start(f32[2048]{0:T(1024)S(1)} %add_rsqrt_fusion) | copy-start | bytes 24580
  14.8 11.9 %copy-start.4 = (bf16[1,2048,512]{2,1,0:T(8,128)(2,1)S(1)}, bf16[1,2048,512]{2,1,0:T(8,128)(2,1)}, u32[]{:S(2)}) copy-start(bf16[1,2048,512]{2,1,0:T(8,128)(2,1)} %param.11) | copy-start | bytes 6291460
  76.0 0.6 copy-start.8
  76.0 1.3 copy-start.6
  127.7 18.1 %copy-start.5 = (bf16[1,2048,512]{2,1,0:T(8,128)(2,1)S(1)}, bf16[1,2048,512]{2,1,0:T(8,128)(2,1)}, u32[]{:S(2)}) copy-start(bf16[1,2048,512]{2,1,0:T(8,128)(2,1)} %param.12) | copy-start | bytes 6291460
  145.8 19.9 %copy-start.3 = (bf16[2,512,3072]{2,1,0:T(8,128)(2,1)S(1)}, bf16[2,512,3072]{2,1,0:T(8,128)(2,1)}, u32[]{:S(2)}) copy-start(bf16[2,512,3072]{2,1,0:T(8,128)(2,1)} %param.13) | copy-start | bytes 18874372
  165.7 10.7 %copy-start.9 = (f32[2048]{0:T(1024)S(1)}, f32[2048]{0:T(1024)}, u32[]{:S(2)}) copy-start(f32[2048]{0:T(1024)} %copy-done.8) | copy-start | bytes 24580
  165.7 10.7 %copy-start.2 = (bf16[1,2048,512]{1,2,0:T(8,128)(2,1)S(1)}, bf16[1,2048,512]{1,2,0:T(8,128)(2,1)}, u32[]{:S(2)}) copy-start(bf16[1,2048,512]{1,2,0:T(8,128)(2,1)} %copy.21) | copy-start | bytes 6291460
  165.7 10.7 %copy-start.7 = (bf16[2048,512]{0,1:T(8,128)(2,1)S(1)}, bf16[2048,512]{0,1:T(8,128)(2,1)}, u32[]{:S(2)}) copy-start(bf16[2048,512]{0,1:T(8,128)(2,1)} %copy-done.6) | copy-start | bytes 6291460
  176.4 12.7 %slice-start.2 = ((s8[6291456]{0:T(1024)(128)(4,1)}), s8[4194304]{0:T(1024)(128)(4,1)S(1)}, s32[]{:S(2)}) async-start(s8[6291456]{0:T(1024)(128)(4,1)} %bitcast.82), calls=%async_computation.3 | async-start | bytes 8388608
  177.8 11.3 %slice-start.3 = ((s8[6291456]{0:T(1024)(128)(4,1)}), s8[2097152]{0:T(1024)(128)(4,1)S(1)}, s32[]{:S(2)}) async-start(s8[6291456]{0:T(1024)(128)(4,1)} %bitcast.82), calls=%async_computation.4 | async-start | bytes 4194304
  216.5 13.2 %copy-start.1 = (bf16[1,2048,512]{1,2,0:T(8,128)(2,1)S(1)}, bf16[1,2048,512]{1,2,0:T(8,128)(2,1)}, u32[]{:S(2)}) copy-start(bf16[1,2048,512]{1,2,0:T(8,128)(2,1)} %copy-done) | copy-start | bytes 6291460
  216.5 13.2 %copy-start.11 = (f32[2048]{0:T(1024)S(1)}, f32[2048]{0:T(1024)}, u32[]{:S(2)}) copy-start(f32[2048]{0:T(1024)} %copy-done.10) | copy-start | bytes 24580
  271.8 260.1 %slice-start = ((s8[6291456]{0:T(1024)(128)(4,1)}), s8[2097152]{0:T(1024)(128)(4,1)S(1)}, s32[]{:S(2)}) async-start(s8[6291456]{0:T(1024)(128)(4,1)} %bitcast.80), calls=%async_computation.1 | async-start | bytes 4194304
  506.2 25.7 %slice-start.1 = ((s8[6291456]{0:T(1024)(128)(4,1)}), s8[4194304]{0:T(1024)(128)(4,1)S(1)}, s32[]{:S(2)}) async-start(s8[6291456]{0:T(1024)(128)(4,1)} %bitcast.80), calls=%async_computation.2 | async-start | bytes 8388608
Sparse Core Ops, SparseCore 0:
  272.0 234.2 all-reduce.2
where the time goes:
time: 589 us; the launch traced here: 581 us
  matrix products  254 us (43%)
  waiting for transfers between devices  234 us (40%)
  other arithmetic  69.5 us (12%)
  between operations  14.7 us (2%)
  local copies, waits for them, and re-layouts  8.48 us (1%)
    psum x1, waiting for transfers between devices, step(): summed[number] = [lax.psum(by_w[name], 'dp') for name in NAMES]  234 us
    dot_general x5, matrix products, layer(): gate = jnp.dot(a, w['w_gate'], preferred_element_type=jnp.float32)  99 us
    dot_general x5, matrix products, layer(): up = jnp.dot(a, w['w_up'], preferred_element_type=jnp.float32)  91.4 us
    convert_element_type x2, other arithmetic, adamw(): return ((w - 0.02 * step).astype(jnp.bfloat16), m, v)  67.7 us
    dot_general x5, matrix products, matmul(): jnp.dot(a, w, preferred_element_type=jnp.float32).astype(jnp.bfloat16)  63.7 us
  transfers between devices with their start and end apart: 1, of which 1 were waited for; matrix products, arithmetic and copies ran while one was open for 0% of the time, Pallas kernels for 0%

commit v1 on v0

v1 whole, which is shorter than its diff:
```python
import functools
import math

import jax
import jax.numpy as jnp
from jax import lax
from jax.experimental import pallas as pl
from jax.experimental.pallas import tpu as pltpu
from jax.sharding import PartitionSpec as P

BLOCK = 512
TILE = 512
SLOTS = 4
STAGES = 8
VMEM_LIMIT = 67_043_328
F32, BF16 = jnp.float32, jnp.bfloat16
NN = (((1,), (0,)), ((), ()))
NT = (((1,), (1,)), ((), ()))


def dot(a, b, dims=NN):
    return lax.dot_general(a, b, dims, preferred_element_type=F32)


def scale_of(wide):
    return lax.rsqrt(jnp.mean(wide * wide, -1, keepdims=True) + 1e-6)


def normed(h):
    wide = h.astype(F32)
    return (wide * scale_of(wide)).astype(BF16)


def train_kernel(
    side, x_hbm, dy_hbm, wg_hbm, wu_hbm, wd_hbm, out_hbm,
    x, a, at, dh, dht, act, dg, du, acc1, acc2, wg, wu, wd,
    grad, r1, r2, part, t1, u1, t2, u2, own, send, recv, w_sem, x_sem, own_sem,
):
    tokens, d = x.shape
    blocks = wg_hbm.shape[2] // BLOCK
    chunks = wg_hbm.shape[0] * blocks
    tiles = tokens // TILE
    half_rows = grad.shape[2] // 2
    n1, n2 = half_rows // side, half_rows // side // side
    cols = BLOCK // 2

    me = lax.axis_index("dp")
    ix, iy = me // side, lax.rem(me, side)

    def turn(i, by):
        return lax.rem(i + (by + side), side)

    along_x = (ix, tuple(turn(ix, s) * side + iy for s in (1, -1)))
    along_y = (iy, tuple(ix * side + turn(iy, s) for s in (1, -1)))
    flows = ((along_x, along_y), (along_y, along_x))
    step_of = (1, -1)

    barrier = pltpu.get_barrier_semaphore()
    for _, near in (along_x, along_y):
        for device in near:
            pl.semaphore_signal(barrier, inc=1, device_id={"dp": device}, device_id_type=pl.DeviceIdType.MESH)

    def rows(flow, s1, s2=None):
        if s2 is None:
            return pl.ds(pl.multiple_of(flow * half_rows + s1 * n1, 16), n1)
        return pl.ds(pl.multiple_of(flow * half_rows + s1 * n1 + s2 * n2, 16), n2)

    def hop(stage, c, flow, way):
        slot = lax.rem(c, SLOTS)
        (i1, near1), (i2, near2) = flows[flow]
        step = step_of[way]
        if stage == 0:
            src, dst, to = grad.at[slot, way, rows(flow, turn(i1, 2)), :], r1.at[slot, flow, way], near1
        elif stage == 1:
            src, dst, to = grad.at[slot, :, rows(flow, turn(i1, step)), :], r2.at[slot, flow, way], near1
        elif stage == 2:
            src, dst, to = t1.at[slot, flow, way], u1.at[slot, flow, way], near2
        elif stage == 3:
            src, dst, to = t2.at[slot, flow, way], u2.at[slot, flow, way], near2
        elif stage == 4:
            src, dst, to = own.at[slot, flow], out_hbm.at[c, :, rows(flow, i1, i2), :], near2
        elif stage == 5:
            src = dst = out_hbm.at[c, way, rows(flow, i1, turn(i2, -step)), :]
            to = near2
        elif stage == 6:
            src = dst = out_hbm.at[c, :, rows(flow, i1), :]
            to = near1
        else:
            src = dst = out_hbm.at[c, way, rows(flow, turn(i1, -step)), :]
            to = near1
        return pltpu.make_async_remote_copy(
            src_ref=src,
            dst_ref=dst,
            send_sem=send.at[slot, stage, flow, way],
            recv_sem=recv.at[slot, stage, flow, way],
            device_id={"dp": to[way]},
            device_id_type=pl.DeviceIdType.MESH,
        )

    def keep(c, flow):
        slot = lax.rem(c, SLOTS)
        (i1, _), (i2, _) = flows[flow]
        return pltpu.make_async_copy(own.at[slot, flow], out_hbm.at[c, :, rows(flow, i1, i2), :], own_sem.at[slot, flow])

    def wait(stage, c):
        for flow in range(2):
            for way in range(2):
                hop(stage, c, flow, way).wait()

    def start(stage, c):
        for flow in range(2):
            for way in range(2):
                hop(stage, c, flow, way).start()

    def advance(event, c):
        slot, pslot = lax.rem(c, SLOTS), lax.rem(c, 2)
        wait(event - 1, c)
        for flow in range(2):
            (i1, _), (i2, _) = flows[flow]
            if event == 1:
                for way in range(2):
                    where = rows(flow, turn(i1, step_of[way]))
                    total = grad[slot, way, where, :].astype(F32) + r1[slot, flow, way].astype(F32)
                    grad[slot, way, where, :] = total.astype(BF16)
            elif event == 2:
                for h in range(2):
                    mine = grad[slot, h, rows(flow, i1), :].astype(F32)
                    part[pslot, flow, h] = mine + r2[slot, flow, 0, h].astype(F32) + r2[slot, flow, 1, h].astype(F32)
                far = pl.ds(pl.multiple_of(turn(i2, 2) * n2, 16), n2)
                for way in range(2):
                    t1[slot, flow, way] = part[pslot, flow, way, far, :].astype(BF16)
            elif event == 3:
                for way in range(2):
                    near = pl.ds(pl.multiple_of(turn(i2, step_of[way]) * n2, 16), n2)
                    for h in range(2):
                        total = part[pslot, flow, h, near, :]
                        if h == way:
                            total = total + u1[slot, flow, way].astype(F32)
                        t2[slot, flow, way, h] = total.astype(BF16)
            elif event == 4:
                here = pl.ds(pl.multiple_of(i2 * n2, 16), n2)
                for h in range(2):
                    total = part[pslot, flow, h, here, :] + u2[slot, flow, 0, h].astype(F32) + u2[slot, flow, 1, h].astype(F32)
                    own[slot, flow, h] = total.astype(BF16)
                keep(c, flow).start()
            elif event == 5:
                keep(c, flow).wait()
        if event < STAGES:
            start(event, c)

    def poll(k, events):
        for behind, event in events:
            c = k - behind

            @pl.when((c >= 0) & (c < chunks))
            def _(c=c, event=event):
                advance(event, c)

    def poll_mid(k):
        poll(k, ((4, 7), (3, 5), (2, 3), (1, 1)))

    def poll_end(k):
        poll(k, ((4, 8), (3, 6), (2, 4), (1, 2)))

    def weights(b):
        layer, j, slot = lax.rem(b // blocks, 2), lax.rem(b, blocks), lax.rem(b, 2)
        span = pl.ds(pl.multiple_of(j * BLOCK, BLOCK), BLOCK)
        return (
            pltpu.make_async_copy(wg_hbm.at[layer, :, span], wg.at[slot], w_sem.at[slot, 0]),
            pltpu.make_async_copy(wu_hbm.at[layer, :, span], wu.at[slot], w_sem.at[slot, 1]),
            pltpu.make_async_copy(wd_hbm.at[layer, span, :], wd.at[slot], w_sem.at[slot, 2]),
        )

    def next_weights(b):
        for copy in weights(b):
            copy.wait()

        @pl.when(b + 1 < 3 * blocks)
        def _():
            for copy in weights(b + 1):
                copy.start()

    def each_tile(body):
        @pl.loop(0, tiles)
        def _(t):
            body(pl.ds(pl.multiple_of(t * TILE, TILE), TILE))

    load_x = pltpu.make_async_copy(x_hbm.at[0], x, x_sem.at[0])
    load_dy = pltpu.make_async_copy(dy_hbm.at[0], dh, x_sem.at[1])
    load_x.start()
    for copy in weights(0):
        copy.start()
    load_dy.start()
    load_x.wait()

    def first(t):
        a[t, :] = normed(x[t, :])
        acc1[t, :] = jnp.zeros((TILE, d), F32)

    each_tile(first)

    @pl.loop(0, blocks)
    def _(b):
        next_weights(b)
        slot = lax.rem(b, 2)

        def forward(t):
            gate = dot(a[t, :], wg[slot])
            up = dot(a[t, :], wu[slot])
            acc1[t, :] += dot((jax.nn.silu(gate) * up).astype(BF16), wd[slot])

        each_tile(forward)

    load_dy.wait()

    def second(t):
        h = (x[t, :].astype(F32) + acc1[t, :].astype(BF16).astype(F32)).astype(BF16)
        x[t, :] = h
        after = normed(h)
        a[t, :] = after
        at[:, t] = after.T
        dht[:, t] = dh[t, :].T
        acc1[t, :] = jnp.zeros((TILE, d), F32)
        acc2[t, :] = jnp.zeros((TILE, d), F32)

    each_tile(second)
    pl.semaphore_wait(barrier, 4)

    def backward(k, to_input):
        next_weights(k + blocks)
        slot, gslot = lax.rem(k + blocks, 2), lax.rem(k, SLOTS)

        def states(t):
            gate = dot(a[t, :], wg[slot])
            up = dot(a[t, :], wu[slot])
            by_act = dot(dh[t, :], wd[slot], NT).astype(BF16).astype(F32)
            s = jax.nn.sigmoid(gate)
            silu = gate * s
            act[t, :] = (silu * up).astype(BF16)
            by_up = (by_act * silu).astype(BF16)
            by_gate = (by_act * up * (s * (1.0 + gate * (1.0 - s)))).astype(BF16)
            dg[t, :] = by_gate
            du[t, :] = by_up
            if to_input:
                acc1[t, :] += dot(by_gate, wg[slot], NT)
                acc2[t, :] += dot(by_up, wu[slot], NT)

        each_tile(states)
        poll_mid(k)
        for h in range(2):
            span = slice(h * cols, (h + 1) * cols)
            grad[gslot, h, 0:d, :] = dot(at[...], dg[:, span]).astype(BF16)
            grad[gslot, h, d : 2 * d, :] = dot(at[...], du[:, span]).astype(BF16)
            grad[gslot, h, 2 * d : 3 * d, :] = dot(dht[...], act[:, span]).astype(BF16)
        start(0, k)
        poll_end(k)

    @pl.loop(0, blocks)
    def _(k):
        backward(k, True)

    again = pltpu.make_async_copy(x_hbm.at[0], act, x_sem.at[0])
    again.start()

    def between(t):
        by_a = (acc1[t, :].astype(BF16).astype(F32) + acc2[t, :].astype(BF16).astype(F32)).astype(BF16).astype(F32)
        wide = x[t, :].astype(F32)
        scale = scale_of(wide)
        along = jnp.sum(by_a * wide, -1, keepdims=True) * (scale * scale * scale / d)
        by_h = (by_a * scale - wide * along).astype(BF16)
        total = (dh[t, :].astype(F32) + by_h.astype(F32)).astype(BF16)
        dh[t, :] = total
        dht[:, t] = total.T

    each_tile(between)
    again.wait()

    def first_again(t):
        before = normed(act[t, :])
        a[t, :] = before
        at[:, t] = before.T

    each_tile(first_again)

    @pl.loop(blocks, 2 * blocks)
    def _(k):
        backward(k, False)

    @pl.loop(2 * blocks, 2 * blocks + 4)
    def _(k):
        poll_mid(k)
        poll_end(k)


def gradients(side, x, dy, wg, wu, wd):
    _, tokens, d = x.shape
    layers, _, ff = wg.shape
    chunks, high, cols = layers * ff // BLOCK, 3 * d, BLOCK // 2
    n1, n2 = high // 2 // side, high // 2 // side // side
    flops = 2 * tokens * d * ff * 17
    vmem = pltpu.VMEM
    return pl.pallas_call(
        functools.partial(train_kernel, side),
        out_shape=jax.ShapeDtypeStruct((chunks, 2, high, cols), BF16),
        in_specs=[pl.BlockSpec(memory_space=pl.ANY)] * 5,
        out_specs=pl.BlockSpec(memory_space=pl.ANY),
        scratch_shapes=[
            vmem((tokens, d), BF16),
            vmem((tokens, d), BF16),
            vmem((d, tokens), BF16),
            vmem((tokens, d), BF16),
            vmem((d, tokens), BF16),
            vmem((tokens, BLOCK), BF16),
            vmem((tokens, BLOCK), BF16),
            vmem((tokens, BLOCK), BF16),
            vmem((tokens, d), F32),
            vmem((tokens, d), F32),
            vmem((2, d, BLOCK), BF16),
            vmem((2, d, BLOCK), BF16),
            vmem((2, BLOCK, d), BF16),
            vmem((SLOTS, 2, high, cols), BF16),
            vmem((SLOTS, 2, 2, n1, cols), BF16),
            vmem((SLOTS, 2, 2, 2, n1, cols), BF16),
            vmem((2, 2, 2, n1, cols), F32),
            vmem((SLOTS, 2, 2, n2, cols), BF16),
            vmem((SLOTS, 2, 2, n2, cols), BF16),
            vmem((SLOTS, 2, 2, 2, n2, cols), BF16),
            vmem((SLOTS, 2, 2, 2, n2, cols), BF16),
            vmem((SLOTS, 2, 2, n2, cols), BF16),
            pltpu.SemaphoreType.DMA((SLOTS, STAGES, 2, 2)),
            pltpu.SemaphoreType.DMA((SLOTS, STAGES, 2, 2)),
            pltpu.SemaphoreType.DMA((2, 3)),
            pltpu.SemaphoreType.DMA((2,)),
            pltpu.SemaphoreType.DMA((SLOTS, 2)),
        ],
        compiler_params=pltpu.CompilerParams(collective_id=0, has_side_effects=True, vmem_limit_bytes=VMEM_LIMIT),
        cost_estimate=pl.CostEstimate(flops=flops, bytes_accessed=4 * wg.size * 3, transcendentals=tokens * ff * 6),
        name="train",
    )(x, dy, wg, wu, wd)


def adamw_kernel(d, g_ref, *refs):
    ins, outs = refs[:9], refs[9:]
    for i in range(3):
        g = g_ref[0, 0, i * d : (i + 1) * d, :]
        g = (g.T if i == 2 else g).astype(F32)
        m = 0.9 * ins[3 + i][0] + 0.1 * g
        v = 0.95 * ins[6 + i][0] + 0.05 * g * g
        w = ins[i][0].astype(F32)
        step = m * lax.rsqrt(v + 1e-8) + 0.1 * w
        outs[i][0] = (w - 0.02 * step).astype(BF16)
        outs[3 + i][0] = m
        outs[6 + i][0] = v


def adamw(g, arrays):
    layers, d, ff = arrays[0].shape
    blocks = ff // BLOCK
    cols = BLOCK // 2

    def across(c, h):
        return layers - 1 - c // blocks, 0, lax.rem(c, blocks) * 2 + h

    def down(c, h):
        return layers - 1 - c // blocks, lax.rem(c, blocks) * 2 + h, 0

    specs = [pl.BlockSpec((1, d, cols), across), pl.BlockSpec((1, d, cols), across), pl.BlockSpec((1, cols, d), down)] * 3
    return pl.pallas_call(
        functools.partial(adamw_kernel, d),
        grid=(g.shape[0], 2),
        out_shape=[jax.ShapeDtypeStruct(one.shape, one.dtype) for one in arrays],
        in_specs=[pl.BlockSpec((1, 1, 3 * d, cols), lambda c, h: (c, h, 0, 0)), *specs],
        out_specs=specs,
        compiler_params=pltpu.CompilerParams(vmem_limit_bytes=60_000_000),
        cost_estimate=pl.CostEstimate(flops=20 * g.size, bytes_accessed=22 * g.size, transcendentals=g.size),
        name="adamw",
    )(g, *arrays)


def solution(mesh):
    side = math.isqrt(mesh.shape["dp"])
    assert side == 4 and side * side == mesh.shape["dp"]

    def step(x, dy, *arrays):
        g = gradients(side, x, dy, *arrays[:3])
        return tuple(adamw(g, arrays))

    return jax.shard_map(
        step,
        mesh=mesh,
        in_specs=(P(("rep", "dp"), None, None),) * 2 + (P(None, None, None),) * 9,
        out_specs=(P("rep", None, None),) * 9,
        check_vma=False,
    )
```

time: 589 us -> 340 us (0.58)
  the two profiles are of different devices: /device:TPU:97 before, /device:TPU:96 now
where the time goes in v1:
time: 340 us
  Pallas kernels  339 us (100%)
    pallas_call x1, Pallas kernels, gradients(): pl.pallas_call(functools.partial(train_kernel, side), out_shape=jax.Shape...  268 us
    pallas_call x1, Pallas kernels, adamw(): pl.pallas_call(functools.partial(adamw_kernel, d), grid=(g.shape[0], 2),...  71.8 us

profile of v1, /device:TPU:96, one launch (start us, length us, event | category | flops | bytes accessed | tf_op | source)
XLA Modules:
  0.0 340.1 jit_solution(8624703608537070749)
XLA Ops:
  0.6 267.5 %train.1.g_ref = bf16[12,2,1536,256]{3,2,1,0:T(8,128)(2,1)} custom-call(bf16[1,2048,512]{2,1,0:T(8,128)(2,1)} %x_hbm.1, bf16[1,2048,512]{2,1,0:T(8,128)(2,1)} %dy_hbm.1, bf16[2,512,3072]{2,1,0:T(8,128)(2,1)} %refs_0_.1, bf16[2,512,3072]{2,1,0:T(8,128)(2,1)} %refs_1_.1, bf16[2,3072,512]{2,1,0:T(8,128)(2,1)} %refs_2_.1), custom_call_target="tpu_custom_call" | custom-call | flops 109521666048 | bytes 37748736 | tf_op jit(solution)/shard_map/train/pallas_call | solution.py:302
  268.2 71.8 %adamw.1 = (bf16[2,512,3072]{2,1,0:T(8,128)(2,1)}, bf16[2,512,3072]{2,1,0:T(8,128)(2,1)}, bf16[2,3072,512]{2,1,0:T(8,128)(2,1)}, f32[2,512,3072]{2,1,0:T(8,128)}...) custom-call(bf16[12,2,1536,256]{3,2,1,0:T(8,128)(2,1)} %train.1.g_re, ...), custom_call_target="tpu_custom_call" | custom-call | flops 188743680 | bytes 207618048 | tf_op jit(solution)/shard_map/adamw/pallas_call | solution.py:368
